TPU v7x, 16 devices: a 4x2x1 block of a 4x4x8 slice. The times are simulated.
16 devices in a mesh: dp: 2 (over y, z), stage: 8 (over x, core).
Axes of the slice: x: 4, y: 2, z: 1, core: 2. Of those that a mesh axis runs over, the one named last changes fastest.
The devices are a block of a 4x4x8 slice.
Arguments:
- token_ids: int32 [64, 128], P('dp'), parts along dimension 0
- label_ids: int32 [64, 128], P('dp'), parts along dimension 0
- embedding: bfloat16 [49152, 576], P('stage')
- w_in: bfloat16 [8, 576, 1536], P('stage')
- w_out: bfloat16 [8, 1536, 576], P('stage')
Outputs:
- output 1: float32 [2], P('dp'), parts along dimension 0
- output 2: float32 [16, 576, 1536], P(('dp', 'stage')), parts along dimension 0
- output 3: float32 [16, 1536, 576], P(('dp', 'stage')), parts along dimension 0
- output 4: float32 [98304, 576], P(('dp', 'stage')), parts along dimension 0
There are 2 independent parts. A program takes and returns all parts, laid end to end along the dimension named above; an argument that names none is the same for every part.
All inputs are finite; a program needn't handle non-finite values.
Results may differ from a plain program's by a relative error of at most 0.0144882.
Values are sent between devices in bfloat16 or wider.
A program may use at most 768 MiB of HBM per device.

v0:
```python
import jax
import jax.numpy as jnp
from jax import lax
from jax.sharding import PartitionSpec as P

NORM_EPS = 1e-6


def norm_f32(act_rows):
    acts_f = act_rows.astype(jnp.float32)
    return acts_f * lax.rsqrt(jnp.mean(acts_f * acts_f, axis=-1, keepdims=True) + NORM_EPS)


def layer_forward(act_rows, w_first, w_second):
    pre_act = jnp.dot(act_rows, w_first, preferred_element_type=jnp.float32)
    hidden = jax.nn.gelu(pre_act).astype(jnp.bfloat16)
    out_f = act_rows.astype(jnp.float32) + jnp.dot(hidden, w_second, preferred_element_type=jnp.float32)
    return out_f.astype(jnp.bfloat16)


def layer_backward(act_rows, grad_out, w_first, w_second):
    pre_act = jnp.dot(act_rows, w_first, preferred_element_type=jnp.float32)
    hidden_f, gelu_pull = jax.vjp(jax.nn.gelu, pre_act)
    hidden = hidden_f.astype(jnp.bfloat16)
    grad_second = jnp.einsum("tf,td->fd", hidden, grad_out, preferred_element_type=jnp.float32)
    grad_hidden = jnp.einsum("td,fd->tf", grad_out, w_second, preferred_element_type=jnp.float32)
    grad_pre = gelu_pull(grad_hidden)[0].astype(jnp.bfloat16)
    grad_first = jnp.einsum("td,tf->df", act_rows, grad_pre, preferred_element_type=jnp.float32)
    grad_in = (grad_out.astype(jnp.float32) + jnp.einsum("tf,df->td", grad_pre, w_first, preferred_element_type=jnp.float32)).astype(jnp.bfloat16)
    return grad_in, grad_first, grad_second


def take_slot(store_arr, mb_slot):
    return lax.dynamic_index_in_dim(store_arr, mb_slot, 0, keepdims=False)


def put_slot(store_arr, new_value, mb_slot, active):
    old_value = lax.dynamic_index_in_dim(store_arr, mb_slot, 0, keepdims=False)
    return lax.dynamic_update_index_in_dim(store_arr, jnp.where(active, new_value, old_value), mb_slot, 0)


def solution(mesh):
    n_stage = mesh.shape["stage"]
    fwd_pairs = [(src_idx, src_idx + 1) for src_idx in range(n_stage - 1)]
    bwd_pairs = [(src_idx + 1, src_idx) for src_idx in range(n_stage - 1)]

    def stage_body(token_ids, label_ids, emb_rows, w_in, w_out):
        stage_idx = lax.axis_index("stage")
        is_first = stage_idx == 0
        is_last = stage_idx == n_stage - 1
        micro_count, micro_tokens = token_ids.shape
        slice_rows, model_dim = emb_rows.shape
        logit_scale = model_dim ** -0.5
        w_first = w_in[0]
        w_second = w_out[0]
        n_ticks = micro_count + n_stage - 1
        row_start = stage_idx * slice_rows
        local_tok = token_ids - row_start
        tok_here = (local_tok >= 0) & (local_tok < slice_rows)
        looked_up = jnp.take(emb_rows, jnp.clip(local_tok, 0, slice_rows - 1), axis=0)
        embedded = lax.psum(jnp.where(tok_here[..., None], looked_up, 0), "stage")
        act_zeros = jnp.zeros((micro_tokens, model_dim), jnp.bfloat16)
        store_zeros = jnp.zeros((micro_count, micro_tokens, model_dim), jnp.bfloat16)

        def fwd_tick(tick_idx, loop_carry):
            incoming, saved_in, last_out = loop_carry
            micro_idx = tick_idx - stage_idx
            active = (micro_idx >= 0) & (micro_idx < micro_count)
            mb_slot = jnp.clip(micro_idx, 0, micro_count - 1)
            act_in = jnp.where(is_first, take_slot(embedded, mb_slot), incoming)
            act_out = lax.cond(active, lambda act_val: layer_forward(act_val, w_first, w_second), lambda act_val: act_val, act_in)
            saved_in = put_slot(saved_in, act_in, mb_slot, active)
            last_out = put_slot(last_out, act_out, mb_slot, active)
            return lax.ppermute(act_out, "stage", fwd_pairs), saved_in, last_out

        _, saved_in, last_out = lax.fori_loop(0, n_ticks, fwd_tick, (act_zeros, store_zeros, store_zeros))

        normed_f, norm_pull = jax.vjp(norm_f32, last_out)
        normed = lax.psum(jnp.where(is_last, normed_f.astype(jnp.bfloat16), 0), "stage")
        local_lab = label_ids - row_start
        vocab_iota = jnp.arange(slice_rows, dtype=jnp.int32)

        def head_step(loop_carry, inputs):
            grad_rows, loss_sum = loop_carry
            normed_mb, lab_mb = inputs
            logits = jnp.einsum("td,vd->tv", normed_mb, emb_rows, preferred_element_type=jnp.float32) * logit_scale
            row_max = lax.pmax(jnp.max(logits, axis=1), "stage")
            exp_logits = jnp.exp(logits - row_max[:, None])
            is_label = lab_mb[:, None] == vocab_iota[None, :]
            row_stats = lax.psum(jnp.stack([jnp.sum(exp_logits, axis=1), jnp.sum(jnp.where(is_label, logits, 0.0), axis=1)]), "stage")
            loss_sum = loss_sum + jnp.sum(jnp.log(row_stats[0]) + row_max - row_stats[1])
            grad_logits = ((exp_logits / row_stats[0][:, None] - is_label.astype(jnp.float32)) * logit_scale).astype(jnp.bfloat16)
            grad_n = lax.psum(jnp.einsum("tv,vd->td", grad_logits, emb_rows, preferred_element_type=jnp.float32), "stage")
            grad_rows = grad_rows + jnp.einsum("tv,td->vd", grad_logits, normed_mb, preferred_element_type=jnp.float32)
            return (grad_rows, loss_sum), grad_n

        head_init = (jnp.zeros((slice_rows, model_dim), jnp.float32), jnp.zeros((), jnp.float32))
        (grad_head, loss_sum), grad_norm = lax.scan(head_step, head_init, (normed, local_lab))
        grad_last = norm_pull(grad_norm)[0]

        def run_layer(operands):
            act_rows, grad_val, acc_a, acc_b = operands
            grad_in, grad_a, grad_b = layer_backward(act_rows, grad_val, w_first, w_second)
            return grad_in, acc_a + grad_a, acc_b + grad_b

        def skip_layer(operands):
            return operands[1], operands[2], operands[3]

        def bwd_tick(tick_idx, loop_carry):
            incoming, acc_first, acc_second, grad_embedded = loop_carry
            micro_idx = tick_idx - (n_stage - 1 - stage_idx)
            active = (micro_idx >= 0) & (micro_idx < micro_count)
            mb_slot = jnp.clip(micro_idx, 0, micro_count - 1)
            grad_out = jnp.where(is_last, take_slot(grad_last, mb_slot), incoming)
            grad_in, acc_first, acc_second = lax.cond(active, run_layer, skip_layer, (take_slot(saved_in, mb_slot), grad_out, acc_first, acc_second))
            grad_embedded = put_slot(grad_embedded, grad_in, mb_slot, active)
            return lax.ppermute(grad_in, "stage", bwd_pairs), acc_first, acc_second, grad_embedded

        bwd_init = (act_zeros, jnp.zeros(w_first.shape, jnp.float32), jnp.zeros(w_second.shape, jnp.float32), store_zeros)
        _, acc_first, acc_second, grad_embedded = lax.fori_loop(0, n_ticks, bwd_tick, bwd_init)

        grad_lookup_in = lax.psum(jnp.where(is_first, grad_embedded, 0), "stage")
        seg_ids = jnp.where(tok_here, local_tok, slice_rows).reshape(-1)
        grad_lookup = jax.ops.segment_sum(grad_lookup_in.reshape(-1, model_dim).astype(jnp.float32), seg_ids, num_segments=slice_rows)
        mean_loss = (loss_sum / (micro_count * micro_tokens)).reshape(1)
        return mean_loss, acc_first[None], acc_second[None], grad_head + grad_lookup

    return jax.shard_map(
        stage_body,
        mesh=mesh,
        in_specs=(P("dp", None), P("dp", None), P("stage", None), P("stage", None, None), P("stage", None, None)),
        out_specs=(P("dp"), P(("dp", "stage"), None, None), P(("dp", "stage"), None, None), P(("dp", "stage"), None)),
        check_vma=False,
    )
```

profile of v0, /device:TPU:117, one launch (start us, length us, event | category | flops | bytes accessed | tf_op | source)
XLA Modules:
  0.0 4397.3 jit_solution(12842280602438771897)
XLA Ops:
  57.0 62.7 %all-reduce.5.cloned.1.call-done = bf16[32,128,576]{1,2,0:T(8,128)(2,1)} async-done(((bf16[32,128,576]{1,2,0:T(8,128)(2,1)}), bf16[32,128,576]{1,2,0:T(8,128)(2,1)}) %all-reduce.5.cloned.1.call-update) | async-done | bytes 4718608 | tf_op jit(solution)/shard_map/psum | solution.py:61
  126.2 443.1 %while.53 = (s32[]{:T(128)}, bf16[128,576]{0,1:T(8,128)(2,1)S(1)}, bf16[32,128,576]{1,2,0:T(8,128)(2,1)}, bf16[32,128,576]{1,2,0:T(8,128)(2,1)}, s32[]{:T(128)},...) while((s32[]{:T(128)}, bf16[128,576]{0,1:T(8,128)(2,1)S(1)}, ...), condition=%wide.region_4.5_spmd, body=%wide.region_1.4_spmd.sunk | while | flops 455196672 | bytes 6488853 | solution.py:76
  585.7 57.4 %all-reduce.7.cloned.1.call-done = bf16[32,128,576]{1,2,0:T(8,128)(2,1)} async-done(((bf16[32,128,576]{1,2,0:T(8,128)(2,1)}), bf16[32,128,576]{1,2,0:T(8,128)(2,1)}) %all-reduce.7.cloned.1.call-update) | async-done | bytes 4718608 | tf_op jit(solution)/shard_map/psum | solution.py:79
  643.1 2880.6 %while.55 = (s32[]{:T(128)}, f32[6144,576]{0,1:T(8,128)}, f32[]{:T(128)}, f32[32,128,576]{1,2,0:T(8,128)}, bf16[32,128,576]{1,2,0:T(8,128)(2,1)}, /*index=5*/bf1...) while((s32[]{:T(128)}, f32[6144,576]{0,1:T(8,128)}, f32[]{:T(128)}, ...), condition=%wide.region_15.16_spmd.clone, body=%wide.region_7.15_spmd.clone.sunk | while | flops 2741576192 | bytes 58013876 | solution.py:98
  687.9 43.8 all-reduce.11.cloned.1.call-done
  779.7 42.0 all-reduce.11.cloned.1.call-done
  869.8 42.0 all-reduce.11.cloned.1.call-done
  959.8 42.0 all-reduce.11.cloned.1.call-done
  1049.7 42.0 all-reduce.11.cloned.1.call-done
  1139.7 42.0 all-reduce.11.cloned.1.call-done
  1229.7 42.0 all-reduce.11.cloned.1.call-done
  1319.8 42.0 all-reduce.11.cloned.1.call-done
  1409.8 42.0 all-reduce.11.cloned.1.call-done
  1499.8 42.0 all-reduce.11.cloned.1.call-done
  1589.8 42.0 all-reduce.11.cloned.1.call-done
  1679.8 42.0 all-reduce.11.cloned.1.call-done
  1949.9 42.0 all-reduce.11.cloned.1.call-done
  2039.8 42.0 all-reduce.11.cloned.1.call-done
  2129.8 42.0 all-reduce.11.cloned.1.call-done
  2219.8 42.0 all-reduce.11.cloned.1.call-done
  2309.8 42.0 all-reduce.11.cloned.1.call-done
  2489.8 42.0 all-reduce.11.cloned.1.call-done
  2579.8 42.0 all-reduce.11.cloned.1.call-done
  2669.8 42.0 all-reduce.11.cloned.1.call-done
  2759.8 42.0 all-reduce.11.cloned.1.call-done
  2849.9 42.0 all-reduce.11.cloned.1.call-done
  3029.8 42.0 all-reduce.11.cloned.1.call-done
  3119.9 42.0 all-reduce.11.cloned.1.call-done
  3209.9 42.0 all-reduce.11.cloned.1.call-done
  3390.0 42.0 all-reduce.11.cloned.1.call-done
  3544.8 695.9 %while.54 = (s32[]{:T(128)}, bf16[128,576]{0,1:T(8,128)(2,1)}, f32[576,1536]{1,0:T(8,128)S(1)}, f32[1536,576]{0,1:T(8,128)}, bf16[32,128,576]{1,2,0:T(8,128)(2,1...) while((s32[]{:T(128)}, bf16[128,576]{0,1:T(8,128)(2,1)}, ...), condition=%wide.region_20.21_spmd, body=%wide.region_17.20_spmd.sunk | while | flops 1140301824 | bytes 61867960 | solution.py:120
  4259.9 68.2 %all-reduce.9.cloned.1.call-done = bf16[4096,576]{0,1:T(8,128)(2,1)} async-done(((bf16[4096,576]{0,1:T(8,128)(2,1)}), bf16[4096,576]{0,1:T(8,128)(2,1)}) %all-reduce.9.cloned.1.call-update) | async-done | bytes 4718608 | tf_op jit(solution)/shard_map/psum | solution.py:122
  (1400 shorter events, 3525.5 us)
Async XLA Ops:
  7.2 112.5 %all-reduce.5.cloned.1.call-start = ((), (), s32[]{:S(2)}) async-start(), calls=%async_computation | async-start | bytes 9437184 | tf_op jit(solution)/shard_map/psum | solution.py:61
  54.2 588.9 %all-reduce.7.cloned.1.call-start = ((), (), s32[]{:S(2)}) async-start(), calls=%async_computation.1 | async-start | bytes 9437184 | tf_op jit(solution)/shard_map/psum | solution.py:79
  643.1 88.6 %all-reduce.11.cloned.1.call-start = ((), (), s32[]{:S(2)}) async-start(), calls=%async_computation.3 | async-start | bytes 589824 | tf_op jit(solution)/shard_map/while/body/eval_jaxpr/psum | solution.py:93
  823.4 88.3 %all-reduce.11.cloned.1.call-start = ((), (), s32[]{:S(2)}) async-start(), calls=%async_computation.3 | async-start | bytes 589824 | tf_op jit(solution)/shard_map/while/body/eval_jaxpr/psum | solution.py:93
  913.4 88.3 %all-reduce.11.cloned.1.call-start = ((), (), s32[]{:S(2)}) async-start(), calls=%async_computation.3 | async-start | bytes 589824 | tf_op jit(solution)/shard_map/while/body/eval_jaxpr/psum | solution.py:93
  1003.4 88.3 %all-reduce.11.cloned.1.call-start = ((), (), s32[]{:S(2)}) async-start(), calls=%async_computation.3 | async-start | bytes 589824 | tf_op jit(solution)/shard_map/while/body/eval_jaxpr/psum | solution.py:93
  1093.4 88.3 %all-reduce.11.cloned.1.call-start = ((), (), s32[]{:S(2)}) async-start(), calls=%async_computation.3 | async-start | bytes 589824 | tf_op jit(solution)/shard_map/while/body/eval_jaxpr/psum | solution.py:93
  1183.4 88.3 %all-reduce.11.cloned.1.call-start = ((), (), s32[]{:S(2)}) async-start(), calls=%async_computation.3 | async-start | bytes 589824 | tf_op jit(solution)/shard_map/while/body/eval_jaxpr/psum | solution.py:93
  1273.4 88.3 %all-reduce.11.cloned.1.call-start = ((), (), s32[]{:S(2)}) async-start(), calls=%async_computation.3 | async-start | bytes 589824 | tf_op jit(solution)/shard_map/while/body/eval_jaxpr/psum | solution.py:93
  1363.5 88.3 %all-reduce.11.cloned.1.call-start = ((), (), s32[]{:S(2)}) async-start(), calls=%async_computation.3 | async-start | bytes 589824 | tf_op jit(solution)/shard_map/while/body/eval_jaxpr/psum | solution.py:93
  1543.5 88.3 %all-reduce.11.cloned.1.call-start = ((), (), s32[]{:S(2)}) async-start(), calls=%async_computation.3 | async-start | bytes 589824 | tf_op jit(solution)/shard_map/while/body/eval_jaxpr/psum | solution.py:93
  1723.5 88.3 %all-reduce.11.cloned.1.call-start = ((), (), s32[]{:S(2)}) async-start(), calls=%async_computation.3 | async-start | bytes 589824 | tf_op jit(solution)/shard_map/while/body/eval_jaxpr/psum | solution.py:93
  1813.5 88.3 %all-reduce.11.cloned.1.call-start = ((), (), s32[]{:S(2)}) async-start(), calls=%async_computation.3 | async-start | bytes 589824 | tf_op jit(solution)/shard_map/while/body/eval_jaxpr/psum | solution.py:93
  1903.5 88.3 %all-reduce.11.cloned.1.call-start = ((), (), s32[]{:S(2)}) async-start(), calls=%async_computation.3 | async-start | bytes 589824 | tf_op jit(solution)/shard_map/while/body/eval_jaxpr/psum | solution.py:93
  1993.5 88.3 %all-reduce.11.cloned.1.call-start = ((), (), s32[]{:S(2)}) async-start(), calls=%async_computation.3 | async-start | bytes 589824 | tf_op jit(solution)/shard_map/while/body/eval_jaxpr/psum | solution.py:93
  2083.5 88.3 %all-reduce.11.cloned.1.call-start = ((), (), s32[]{:S(2)}) async-start(), calls=%async_computation.3 | async-start | bytes 589824 | tf_op jit(solution)/shard_map/while/body/eval_jaxpr/psum | solution.py:93
  2173.5 88.3 %all-reduce.11.cloned.1.call-start = ((), (), s32[]{:S(2)}) async-start(), calls=%async_computation.3 | async-start | bytes 589824 | tf_op jit(solution)/shard_map/while/body/eval_jaxpr/psum | solution.py:93
  2263.5 88.3 %all-reduce.11.cloned.1.call-start = ((), (), s32[]{:S(2)}) async-start(), calls=%async_computation.3 | async-start | bytes 589824 | tf_op jit(solution)/shard_map/while/body/eval_jaxpr/psum | solution.py:93
  2353.5 88.3 %all-reduce.11.cloned.1.call-start = ((), (), s32[]{:S(2)}) async-start(), calls=%async_computation.3 | async-start | bytes 589824 | tf_op jit(solution)/shard_map/while/body/eval_jaxpr/psum | solution.py:93
  2443.5 88.3 %all-reduce.11.cloned.1.call-start = ((), (), s32[]{:S(2)}) async-start(), calls=%async_computation.3 | async-start | bytes 589824 | tf_op jit(solution)/shard_map/while/body/eval_jaxpr/psum | solution.py:93
  2533.5 88.3 %all-reduce.11.cloned.1.call-start = ((), (), s32[]{:S(2)}) async-start(), calls=%async_computation.3 | async-start | bytes 589824 | tf_op jit(solution)/shard_map/while/body/eval_jaxpr/psum | solution.py:93
  2623.5 88.3 %all-reduce.11.cloned.1.call-start = ((), (), s32[]{:S(2)}) async-start(), calls=%async_computation.3 | async-start | bytes 589824 | tf_op jit(solution)/shard_map/while/body/eval_jaxpr/psum | solution.py:93
  2713.5 88.3 %all-reduce.11.cloned.1.call-start = ((), (), s32[]{:S(2)}) async-start(), calls=%async_computation.3 | async-start | bytes 589824 | tf_op jit(solution)/shard_map/while/body/eval_jaxpr/psum | solution.py:93
  2803.5 88.3 %all-reduce.11.cloned.1.call-start = ((), (), s32[]{:S(2)}) async-start(), calls=%async_computation.3 | async-start | bytes 589824 | tf_op jit(solution)/shard_map/while/body/eval_jaxpr/psum | solution.py:93
  2893.5 88.3 %all-reduce.11.cloned.1.call-start = ((), (), s32[]{:S(2)}) async-start(), calls=%async_computation.3 | async-start | bytes 589824 | tf_op jit(solution)/shard_map/while/body/eval_jaxpr/psum | solution.py:93
  2983.5 88.3 %all-reduce.11.cloned.1.call-start = ((), (), s32[]{:S(2)}) async-start(), calls=%async_computation.3 | async-start | bytes 589824 | tf_op jit(solution)/shard_map/while/body/eval_jaxpr/psum | solution.py:93
  3073.5 88.3 %all-reduce.11.cloned.1.call-start = ((), (), s32[]{:S(2)}) async-start(), calls=%async_computation.3 | async-start | bytes 589824 | tf_op jit(solution)/shard_map/while/body/eval_jaxpr/psum | solution.py:93
  3163.5 88.3 %all-reduce.11.cloned.1.call-start = ((), (), s32[]{:S(2)}) async-start(), calls=%async_computation.3 | async-start | bytes 589824 | tf_op jit(solution)/shard_map/while/body/eval_jaxpr/psum | solution.py:93
  3253.6 88.3 %all-reduce.11.cloned.1.call-start = ((), (), s32[]{:S(2)}) async-start(), calls=%async_computation.3 | async-start | bytes 589824 | tf_op jit(solution)/shard_map/while/body/eval_jaxpr/psum | solution.py:93
  3343.6 88.3 %all-reduce.11.cloned.1.call-start = ((), (), s32[]{:S(2)}) async-start(), calls=%async_computation.3 | async-start | bytes 589824 | tf_op jit(solution)/shard_map/while/body/eval_jaxpr/psum | solution.py:93
  3433.7 88.3 %all-reduce.11.cloned.1.call-start = ((), (), s32[]{:S(2)}) async-start(), calls=%async_computation.3 | async-start | bytes 589824 | tf_op jit(solution)/shard_map/while/body/eval_jaxpr/psum | solution.py:93
  3523.7 804.4 %all-reduce.9.cloned.1.call-start = ((), (), s32[]{:S(2)}) async-start(), calls=%async_computation.2 | async-start | bytes 9437184 | tf_op jit(solution)/shard_map/psum | solution.py:122
  (183 other events, 1145.7 us)
Sparse Core Ops, SparseCore 0:
  54.3 65.3 all-reduce.4
  577.6 65.5 all-reduce.6
  768.8 52.8 all-reduce.10
  858.8 52.8 all-reduce.10
  948.9 52.8 all-reduce.10
  1038.9 52.8 all-reduce.10
  1128.9 52.8 all-reduce.10
  1218.9 52.8 all-reduce.10
  1308.9 52.8 all-reduce.10
  1398.9 52.8 all-reduce.10
  1488.9 52.8 all-reduce.10
  1578.9 52.8 all-reduce.10
  1669.0 52.8 all-reduce.10
  1759.0 52.8 all-reduce.10
  1849.0 52.8 all-reduce.10
  1939.0 52.8 all-reduce.10
  2028.9 52.8 all-reduce.10
  2118.9 52.8 all-reduce.10
  2209.0 52.8 all-reduce.10
  2479.0 52.8 all-reduce.10
  2569.0 52.8 all-reduce.10
  2659.0 52.8 all-reduce.10
  2749.0 52.8 all-reduce.10
  2839.0 52.8 all-reduce.10
  2929.0 52.8 all-reduce.10
  3019.0 52.8 all-reduce.10
  3109.0 52.8 all-reduce.10
  3199.0 52.8 all-reduce.10
  3289.1 52.8 all-reduce.10
  3379.1 52.8 all-reduce.10
  3469.1 52.8 all-reduce.10
  4244.1 83.9 all-reduce.8
  (3 shorter events, 158.0 us)
where the time goes:
time: 4420 us; the launch traced here: 4400 us
  waiting for transfers between devices  1690 us (38%)
  matrix products  1030 us (23%)
  blocking collectives  761 us (17%)
  local copies, waits for them, and re-layouts  356 us (8%)
  other arithmetic  317 us (7%)
  starting transfers between devices  198 us (4%)
    psum x32, waiting for transfers between devices, head_step(): lax.psum(jnp.einsum('tv,vd->td', grad_logits, emb_rows, preferred_element...  1350 us
    psum x32, blocking collectives, head_step(): lax.psum(jnp.stack([jnp.sum(exp_logits, axis=1), jnp.sum(jnp.where(is_lab...  400 us
    pmax x32, blocking collectives, head_step(): row_max = lax.pmax(jnp.max(logits, axis=1), 'stage')  361 us
    dot_general x32, matrix products, head_step(): jnp.einsum('tv,td->vd', grad_logits, normed_mb, preferred_element_type=jn...  309 us
    dot_general x32, matrix products, head_step(): jnp.einsum('tv,vd->td', grad_logits, emb_rows, preferred_element_type=jnp...  189 us
    dynamic_update_slice x117, other arithmetic, put_slot(): lax.dynamic_update_index_in_dim(store_arr, jnp.where(active, new_value, o...  157 us
    dot_general x32, matrix products, head_step(): jnp.einsum('td,vd->tv', normed_mb, emb_rows, preferred_element_type=jnp.f...  147 us
    dynamic_slice x117, local copies, waits for them, and re-layouts, put_slot(): old_value = lax.dynamic_index_in_dim(store_arr, mb_slot, 0, keepdims=False)  134 us
  transfers between devices with their start and end apart: 113, of which 109 were waited for; matrix products, arithmetic and copies ran while one was open for 12% of the time, Pallas kernels for 0%

commit v1 on v0

v1 whole, which is shorter than its diff:
```python
import functools

import jax
import jax.numpy as jnp
from jax import lax
from jax.experimental import pallas as pl
from jax.experimental.pallas import tpu as pltpu
from jax.sharding import PartitionSpec as P

NORM_EPS = 1e-6
MESH = pl.DeviceIdType.MESH
VMEM_BYTES = 66_000_000
FWD_ROWS = 128
BWD_ROWS = 256
HEAD_ROWS = 512
HEAD_COLS = 1024
SCATTER_ROWS = 512
GELU_K = 0.7978845608028654
GELU_C = 0.044715


def full_vmem():
    return pl.BlockSpec(memory_space=pltpu.VMEM)


def any_space():
    return pl.BlockSpec(memory_space=pl.ANY)


def remote(src, dst, send_sem, recv_sem, dev):
    return pltpu.make_async_remote_copy(
        src_ref=src, dst_ref=dst, send_sem=send_sem, recv_sem=recv_sem, device_id={"stage": dev}, device_id_type=MESH
    )


def group_barrier(me, n):
    barrier = pltpu.get_barrier_semaphore()
    for step in range(1, n):
        pl.semaphore_signal(barrier, inc=1, device_id={"stage": lax.rem(me + step, n)}, device_id_type=MESH)
    pl.semaphore_wait(barrier, n - 1)


def dot_nt(a, b):
    return lax.dot_general(a, b, (((1,), (1,)), ((), ())), preferred_element_type=jnp.float32)


def dot_tn(a, b):
    return lax.dot_general(a, b, (((0,), (0,)), ((), ())), preferred_element_type=jnp.float32)


def fwd_kernel(
    n, rows, w1, w2, xin_out, xl_out, h_out, dg_out,
    xin, xl, ea, eb, ec, es, y, hb, gb,
    e_send, ea_recv, eb_recv, ec_recv, f_send, x_recv, b_send, b_recv, h_sem, g_sem, o_sem,
):
    me = lax.axis_index("stage")
    size = FWD_ROWS
    count = rows.shape[0] // size
    last = n - 1
    odd = lax.rem(me, 2) == 1
    relay = odd & (me < last)
    group_barrier(me, n)

    def sl(c):
        return pl.ds(pl.multiple_of(c * size, size), size)

    def odd_send(c):
        return remote(rows.at[sl(c)], ea.at[sl(c)], e_send.at[c], ea_recv.at[c], me - 1)

    def even_send(c, dst, recv, dev):
        return remote(es.at[sl(c)], dst.at[sl(c)], e_send.at[c], recv.at[c], dev)

    def combine_and_send(c, has_eb, dst, recv, dev):
        even_send(c, ea, ea_recv, me).wait_recv()
        total = rows[sl(c), :] + ea[sl(c), :]
        if has_eb:
            even_send(c, eb, eb_recv, me).wait_recv()
            total = total + eb[sl(c), :]
        es[sl(c), :] = total
        even_send(c, dst, recv, dev).start()

    lead = 6

    @pl.when(odd)
    def _():
        @pl.loop(0, count)
        def _(c):
            odd_send(c).start()

    @pl.when(me == 4)
    def _():
        @pl.loop(0, count)
        def _(c):
            combine_and_send(c, False, eb, eb_recv, 2)

    @pl.when(me == 6)
    def _():
        @pl.loop(0, count)
        def _(c):
            combine_and_send(c, False, ec, ec_recv, 0)

    @pl.when(me == 2)
    def _():
        @pl.loop(0, lead)
        def _(c):
            combine_and_send(c, True, eb, eb_recv, 0)

    def fwd_send(c):
        return remote(y.at[sl(c)], xin.at[sl(c)], f_send.at[c], x_recv.at[c], me + 1)

    def bcast(src, c, which, dev):
        return remote(src.at[sl(c)], xl.at[sl(c)], b_send.at[which, c], b_recv.at[c], dev)

    def h_copy(c, slot):
        return pltpu.make_async_copy(hb.at[slot], h_out.at[sl(c)], h_sem.at[slot])

    def g_copy(c, slot):
        return pltpu.make_async_copy(gb.at[slot], dg_out.at[sl(c)], g_sem.at[slot])

    def layer(c):
        slot = lax.rem(c, 2)

        @pl.when(me == 0)
        def _():
            even_send(c, ea, ea_recv, me).wait_recv()
            even_send(c, eb, eb_recv, me).wait_recv()
            even_send(c, ec, ec_recv, me).wait_recv()
            xin[sl(c), :] = (rows[sl(c), :] + ea[sl(c), :]) + (eb[sl(c), :] + ec[sl(c), :])

        @pl.when(me > 0)
        def _():
            remote(y.at[sl(c)], xin.at[sl(c)], f_send.at[c], x_recv.at[c], me).wait_recv()

        @pl.when(c >= 2)
        def _():
            h_copy(c - 2, slot).wait()
            g_copy(c - 2, slot).wait()

        x = xin[sl(c), :]
        pre = jnp.dot(x, w1[...], preferred_element_type=jnp.float32)
        sq = pre * pre
        th = jnp.tanh(GELU_K * (pre + GELU_C * (pre * sq)))
        cdf = 0.5 * (1.0 + th)
        hidden = (pre * cdf).astype(jnp.bfloat16)
        gb[slot] = cdf + (0.5 * pre) * (1.0 - th * th) * (GELU_K + (3.0 * GELU_K * GELU_C) * sq)
        hb[slot] = hidden
        out = x.astype(jnp.float32) + jnp.dot(hidden, w2[...], preferred_element_type=jnp.float32)
        y[sl(c), :] = out.astype(jnp.bfloat16)

        @pl.when(me < last)
        def _():
            fwd_send(c).start()

        @pl.when(me == last)
        def _():
            bcast(y, c, 0, last - 1).start()

            @pl.when(lax.rem(c, 2) == 0)
            def _():
                bcast(y, c, 1, 1).start()

            @pl.when(lax.rem(c, 2) == 1)
            def _():
                bcast(y, c, 1, last - 2).start()

        h_copy(c, slot).start()
        g_copy(c, slot).start()

    def has_next(c):
        up = lax.rem(c, 2) == 0
        return (up & (me < last - 2)) | (jnp.logical_not(up) & (me > 1))

    def next_relay(c):
        return me + 2 - 4 * lax.rem(c, 2)

    def relay_step(c):
        bcast(xl, c, 0, me).wait_recv()
        bcast(xl, c, 0, me - 1).start()

        @pl.when(has_next(c))
        def _():
            bcast(xl, c, 1, next_relay(c)).start()

    lag = (last - me) * 2 + 4

    @pl.loop(0, count + 2 * last + 4)
    def _(i):
        @pl.when((me == 2) & (i + lead < count))
        def _():
            combine_and_send(i + lead, True, eb, eb_recv, 0)

        @pl.when(i < count)
        def _():
            layer(i)

        @pl.when(relay & (i >= lag) & (i - lag < count))
        def _():
            relay_step(i - lag)

    @pl.when(jnp.logical_not(odd))
    def _():
        @pl.loop(0, count)
        def _(c):
            bcast(xl, c, 0, me).wait_recv()

    @pl.when(me == last)
    def _():
        xl[...] = y[...]

    copy_xin = pltpu.make_async_copy(xin, xin_out, o_sem.at[0])
    copy_xl = pltpu.make_async_copy(xl, xl_out, o_sem.at[1])
    copy_xin.start()
    copy_xl.start()

    @pl.loop(0, count)
    def _(c):
        @pl.when(odd)
        def _():
            odd_send(c).wait_send()

        @pl.when(jnp.logical_not(odd) & (me > 0))
        def _():
            even_send(c, eb, eb_recv, me).wait_send()

        @pl.when(me < last)
        def _():
            fwd_send(c).wait_send()

        @pl.when(odd)
        def _():
            bcast(xl, c, 0, me).wait_send()

        @pl.when((me == last) | (relay & has_next(c)))
        def _():
            bcast(xl, c, 1, me).wait_send()

    for c in (count - 2, count - 1):
        h_copy(c, c % 2).wait()
        g_copy(c, c % 2).wait()
    copy_xin.wait()
    copy_xl.wait()


def head_kernel(
    n, xl, emb, lab, det, gl, loss,
    nblk, ntr, probs, mt, st, labsum, cmat, gn, gsend, gr, gst, sstat, rstat,
    s_send, s_recv, g_send, g_recv, l_send, l_recv,
):
    me = lax.axis_index("stage")
    last = n - 1
    tokens, dim = xl.shape
    slice_rows = emb.shape[0]
    size, cols = HEAD_ROWS, HEAD_COLS
    blocks, tiles = tokens // size, slice_rows // cols
    own = size // n
    scale = dim ** -0.5
    group_barrier(me, n)
    lane = lax.broadcasted_iota(jnp.int32, (size, 128), 1)

    def sl(b):
        return pl.ds(pl.multiple_of(b * size, size), size)

    def tile(j):
        return pl.ds(pl.multiple_of(j * cols, cols), cols)

    def own_rows(b, dev):
        return pl.ds(pl.multiple_of(b * size + dev * own, own), own)

    def peer(step):
        return lax.rem(me + step, n)

    def stat_send(b, dev):
        return remote(sstat.at[b], rstat.at[b, me], s_send.at[b, dev], s_recv.at[b, me], dev)

    def stat_recv(b, dev):
        return remote(sstat.at[b], rstat.at[b, dev], s_send.at[b, dev], s_recv.at[b, dev], me)

    def grad_piece(b, dev):
        return gsend.at[lax.rem(b, 2), pl.ds(pl.multiple_of(dev * own, own), own)]

    def grad_send(b, dev):
        return remote(grad_piece(b, dev), gr.at[b, me], g_send.at[b, dev], g_recv.at[b, me], dev)

    def grad_recv(b, dev):
        return remote(grad_piece(b, dev), gr.at[b, dev], g_send.at[b, dev], g_recv.at[b, dev], me)

    def last_send(b):
        return remote(gst.at[b], gl.at[own_rows(b, me)], l_send.at[b], l_recv.at[b, me], last)

    def last_recv(b, dev):
        return remote(gst.at[b], gl.at[own_rows(b, dev)], l_send.at[b], l_recv.at[b, dev], me)

    def last_copy(b):
        return pltpu.make_async_copy(gst.at[b], gl.at[own_rows(b, me)], l_send.at[b])

    def label_mask(b, j):
        ids = lax.broadcasted_iota(jnp.int32, (size, cols), 1)
        return ids == (lab[sl(b), :] - j * cols)

    def open_block(b):
        acts = xl[sl(b), :].astype(jnp.float32)
        normed = acts * lax.rsqrt(jnp.mean(acts * acts, axis=-1, keepdims=True) + NORM_EPS)
        nblk[...] = normed.astype(jnp.bfloat16)
        ntr[lax.rem(b, 3)] = normed.T.astype(jnp.bfloat16)
        mt[lax.rem(b, 3)] = jnp.full((size, 128), -jnp.inf, jnp.float32)
        st[...] = jnp.zeros((size, 128), jnp.float32)
        labsum[...] = jnp.zeros((size, 128), jnp.float32)

    def logits_tile(b, j):
        logits = dot_nt(nblk[...], emb[tile(j), :])
        row_max = jnp.max(logits, axis=1, keepdims=True)
        exps = jnp.exp((logits - row_max) * scale)
        probs[lax.rem(b, 2), :, tile(j)] = exps.astype(jnp.bfloat16)
        here = lane == j
        mt[lax.rem(b, 3)] = jnp.where(here, row_max, mt[lax.rem(b, 3)])
        st[...] = jnp.where(here, jnp.sum(exps, axis=1, keepdims=True), st[...])
        labsum[...] += jnp.sum(jnp.where(label_mask(b, j), logits, 0.0), axis=1, keepdims=True)

    def close_block(b):
        tile_max = mt[lax.rem(b, 3)]
        row_max = jnp.max(tile_max, axis=1, keepdims=True)
        row_sum = jnp.sum(st[...] * jnp.exp((tile_max - row_max) * scale), axis=1, keepdims=True)
        packed = jnp.where(lane == 0, row_max, jnp.where(lane == 1, row_sum, labsum[...]))
        rows = packed.T[:8]
        sstat[b] = rows
        rstat[b, me] = rows
        for step in range(1, n):
            stat_send(b, peer(step)).start()

    def join_stats(b):
        for step in range(1, n):
            stat_recv(b, peer(step)).wait_recv()
        parts = [rstat[b, dev] for dev in range(n)]
        row_max = functools.reduce(jnp.maximum, [part[0:1] for part in parts])
        row_sum = sum(part[1:2] * jnp.exp((part[0:1] - row_max) * scale) for part in parts)
        row_lab = sum(part[2:3] for part in parts)
        lse = row_max * scale + jnp.log(row_sum)
        loss[...] += jnp.sum(lse - row_lab * scale)
        lse_cols = jnp.broadcast_to(lse, (128, size)).T
        cmat[...] = jnp.exp(mt[lax.rem(b, 3)] * scale - lse_cols) * scale
        gn[...] = jnp.zeros_like(gn)

    def grad_tile(b, j):
        factor = jnp.sum(jnp.where(lane == j, cmat[...], 0.0), axis=1, keepdims=True)
        exps = probs[lax.rem(b, 2), :, tile(j)].astype(jnp.float32)
        dlog = (exps * factor - jnp.where(label_mask(b, j), scale, 0.0)).astype(jnp.bfloat16)
        gn[...] += jnp.dot(dlog, emb[tile(j), :], preferred_element_type=jnp.float32)
        det[:, tile(j)] += jnp.dot(ntr[lax.rem(b, 3)], dlog, preferred_element_type=jnp.float32)

    def wait_grad_sends(b):
        for step in range(1, n):
            grad_send(b, peer(step)).wait_send()

    def send_grads(b):
        if isinstance(b, int):
            if b >= 2:
                wait_grad_sends(b - 2)
        else:
            @pl.when(b >= 2)
            def _():
                wait_grad_sends(b - 2)
        gsend[lax.rem(b, 2)] = gn[...].astype(jnp.bfloat16)
        gr[b, me] = gn[pl.ds(pl.multiple_of(me * own, own), own), :].astype(jnp.bfloat16)
        for step in range(1, n):
            grad_send(b, peer(step)).start()

    def own_block(b):
        for step in range(1, n):
            grad_recv(b, peer(step)).wait_recv()
        grad = sum(gr[b, dev].astype(jnp.float32) for dev in range(n))
        acts = xl[own_rows(b, me), :].astype(jnp.float32)
        inv = lax.rsqrt(jnp.mean(acts * acts, axis=-1, keepdims=True) + NORM_EPS)
        normed = acts * inv
        out = inv * (grad - normed * jnp.mean(grad * normed, axis=-1, keepdims=True))
        gst[b] = out.astype(jnp.bfloat16)

        @pl.when(me < last)
        def _():
            last_send(b).start()

        @pl.when(me == last)
        def _():
            last_copy(b).start()

    det[...] = jnp.zeros_like(det)
    loss[...] = jnp.zeros_like(loss)

    @pl.loop(0, 2)
    def _(b):
        open_block(b)

        @pl.loop(0, tiles)
        def _(j):
            logits_tile(b, j)

        close_block(b)

    @pl.loop(2, blocks)
    def _(b):
        join_stats(b - 2)
        open_block(b)

        @pl.loop(0, tiles)
        def _(j):
            grad_tile(b - 2, j)
            logits_tile(b, j)

        close_block(b)

        @pl.when(b >= 3)
        def _():
            own_block(b - 3)

        send_grads(b - 2)

    @pl.loop(blocks - 2, blocks)
    def _(b):
        join_stats(b)

        @pl.loop(0, tiles)
        def _(j):
            grad_tile(b, j)

        own_block(b - 1)
        send_grads(b)

    own_block(blocks - 1)

    @pl.loop(0, blocks)
    def _(b):
        for step in range(1, n):
            stat_send(b, peer(step)).wait_send()

        @pl.when(b >= blocks - 2)
        def _():
            wait_grad_sends(b)

        @pl.when(me < last)
        def _():
            last_send(b).wait_send()

        @pl.when(me == last)
        def _():
            last_copy(b).wait()
            for dev in range(n - 1):
                last_recv(b, dev).wait_recv()


def bwd_kernel(
    n, gl, xin, h_in, dg_in, w1, w2, dw1, dw2t, gx_out,
    gin, gout, gall, hb, gb,
    f_send, g_recv, b_send, b_recv, h_sem, d_sem, o_sem,
):
    me = lax.axis_index("stage")
    last = n - 1
    size = BWD_ROWS
    count = xin.shape[0] // size
    odd = lax.rem(me, 2) == 1
    relay = jnp.logical_not(odd) & (me > 0)
    group_barrier(me, n)

    def sl(c):
        return pl.ds(pl.multiple_of(c * size, size), size)

    def h_copy(c):
        slot = lax.rem(c, 2)
        return pltpu.make_async_copy(h_in.at[sl(c)], hb.at[slot], h_sem.at[slot])

    def d_copy(c):
        slot = lax.rem(c, 2)
        return pltpu.make_async_copy(dg_in.at[sl(c)], gb.at[slot], d_sem.at[slot])

    def grad_send(c, dev):
        return remote(gout.at[sl(c)], gin.at[sl(c)], f_send.at[c], g_recv.at[c], dev)

    def bcast(src, c, which, dev):
        return remote(src.at[sl(c)], gall.at[sl(c)], b_send.at[which, c], b_recv.at[c], dev)

    h_copy(0).start()
    d_copy(0).start()
    dw1[...] = jnp.zeros_like(dw1)
    dw2t[...] = jnp.zeros_like(dw2t)

    @pl.when(me == last)
    def _():
        whole = pltpu.make_async_copy(gl, gin, o_sem.at[0])
        whole.start()
        whole.wait()

    def layer(c):
        slot = lax.rem(c, 2)

        @pl.when(c + 1 < count)
        def _():
            h_copy(c + 1).start()
            d_copy(c + 1).start()

        h_copy(c).wait()
        d_copy(c).wait()

        @pl.when(me < last)
        def _():
            grad_send(c, me).wait_recv()

        grad = gin[sl(c), :]
        grad_hidden = dot_nt(grad, w2[...])
        grad_pre = (grad_hidden * gb[slot]).astype(jnp.bfloat16)
        grad_in = grad.astype(jnp.float32) + dot_nt(grad_pre, w1[...])
        gout[sl(c), :] = grad_in.astype(jnp.bfloat16)

        @pl.when(me > 0)
        def _():
            grad_send(c, me - 1).start()

        @pl.when(me == 0)
        def _():
            bcast(gout, c, 0, 1).start()
            bcast(gout, c, 1, 2).start()
            bcast(gout, c, 2, last - 1).start()

        dw1[...] += dot_tn(xin[sl(c), :], grad_pre)
        dw2t[...] += dot_tn(grad, hb[slot])

    def relay_step(c):
        bcast(gall, c, 0, me).wait_recv()
        bcast(gall, c, 0, me + 1).start()

        @pl.when(me == 2)
        def _():
            bcast(gall, c, 1, 4).start()

    lag = me + 2

    @pl.loop(0, count + n)
    def _(i):
        @pl.when(i < count)
        def _():
            layer(i)

        @pl.when(relay & (i >= lag) & (i - lag < count))
        def _():
            relay_step(i - lag)

    @pl.when(odd)
    def _():
        @pl.loop(0, count)
        def _(c):
            bcast(gall, c, 0, me).wait_recv()

    @pl.when(me == 0)
    def _():
        whole = pltpu.make_async_copy(gout, gx_out, o_sem.at[0])
        whole.start()
        whole.wait()

    @pl.when(me > 0)
    def _():
        whole = pltpu.make_async_copy(gall, gx_out, o_sem.at[0])
        whole.start()
        whole.wait()

    @pl.loop(0, count)
    def _(c):
        @pl.when(me > 0)
        def _():
            grad_send(c, me).wait_send()

        @pl.when(jnp.logical_not(odd))
        def _():
            bcast(gall, c, 0, me).wait_send()

        @pl.when((me == 0) | (me == 2))
        def _():
            bcast(gall, c, 1, me).wait_send()

        @pl.when(me == 0)
        def _():
            bcast(gall, c, 2, me).wait_send()


def scatter_kernel(starts, ids, pos, det, gx, out, grads):
    blk = pl.program_id(0)

    @pl.when(blk == 0)
    def _():
        grads[...] = gx[...].astype(jnp.float32)

    out[...] = det[...].T
    base = blk * SCATTER_ROWS

    def add_row(k, carry):
        row = pl.ds(ids[k] - base, 1)
        out[row, :] = out[row, :] + grads[pl.ds(pos[k], 1), :]
        return carry

    lax.fori_loop(starts[blk], starts[blk + 1], add_row, 0)


def comm_params(collective_id):
    return pltpu.CompilerParams(collective_id=collective_id, has_side_effects=True, vmem_limit_bytes=VMEM_BYTES)


def solution(mesh):
    n = mesh.shape["stage"]
    bf16, f32 = jnp.bfloat16, jnp.float32
    dma = pltpu.SemaphoreType.DMA
    shape = jax.ShapeDtypeStruct

    def stage_body(token_ids, label_ids, emb_rows, w_in, w_out):
        stage_idx = lax.axis_index("stage")
        micro_count, micro_tokens = token_ids.shape
        tokens = micro_count * micro_tokens
        slice_rows, dim = emb_rows.shape
        w1, w2 = w_in[0], w_out[0]
        ffn = w1.shape[1]
        row_start = stage_idx * slice_rows

        local_tok = token_ids.reshape(tokens) - row_start
        tok_here = (local_tok >= 0) & (local_tok < slice_rows)
        looked_up = jnp.take(emb_rows, jnp.clip(local_tok, 0, slice_rows - 1), axis=0)
        rows = jnp.where(tok_here[:, None], looked_up, 0)
        local_lab = label_ids.reshape(tokens, 1) - row_start

        keys = jnp.where(tok_here, local_tok, slice_rows)
        sorted_ids, sorted_pos = lax.sort((keys, lax.iota(jnp.int32, tokens)), num_keys=1, is_stable=False)
        edges = lax.iota(jnp.int32, slice_rows // SCATTER_ROWS + 1) * SCATTER_ROWS
        starts = jnp.sum((keys[None, :] < edges[:, None]).astype(jnp.int32), axis=1)

        size, count = FWD_ROWS, tokens // FWD_ROWS
        big = pltpu.VMEM((tokens, dim), bf16)
        xin, xl, hidden, dgelu = pl.pallas_call(
            functools.partial(fwd_kernel, n),
            name="forward",
            out_shape=[shape((tokens, dim), bf16), shape((tokens, dim), bf16), shape((tokens, ffn), bf16), shape((tokens, ffn), f32)],
            in_specs=[full_vmem()] * 3,
            out_specs=[any_space()] * 4,
            scratch_shapes=[big] * 7
            + [pltpu.VMEM((2, size, ffn), bf16), pltpu.VMEM((2, size, ffn), f32)]
            + [dma((count,))] * 6
            + [dma((2, count)), dma((count,)), dma((2,)), dma((2,)), dma((2,))],
            compiler_params=comm_params(1),
        )(rows, w1, w2)

        blocks = tokens // HEAD_ROWS
        own = HEAD_ROWS // n
        stat = pltpu.VMEM((HEAD_ROWS, 128), f32)
        det, gl, loss = pl.pallas_call(
            functools.partial(head_kernel, n),
            name="head",
            out_shape=[shape((dim, slice_rows), f32), shape((tokens, dim), bf16), shape((8, 128), f32)],
            in_specs=[full_vmem()] * 3,
            out_specs=[full_vmem(), any_space(), full_vmem()],
            scratch_shapes=[
                pltpu.VMEM((HEAD_ROWS, dim), bf16),
                pltpu.VMEM((3, dim, HEAD_ROWS), bf16),
                pltpu.VMEM((2, HEAD_ROWS, slice_rows), bf16),
                pltpu.VMEM((3, HEAD_ROWS, 128), f32),
                stat, stat, stat,
                pltpu.VMEM((HEAD_ROWS, dim), f32),
                pltpu.VMEM((2, HEAD_ROWS, dim), bf16),
                pltpu.VMEM((blocks, n, own, dim), bf16),
                pltpu.VMEM((blocks, own, dim), bf16),
                pltpu.VMEM((blocks, 8, HEAD_ROWS), f32),
                pltpu.VMEM((blocks, n, 8, HEAD_ROWS), f32),
            ]
            + [dma((blocks, n))] * 4
            + [dma((blocks,)), dma((blocks, n))],
            compiler_params=comm_params(2),
        )(xl, emb_rows, local_lab)

        size, count = BWD_ROWS, tokens // BWD_ROWS
        dw1, dw2t, gx = pl.pallas_call(
            functools.partial(bwd_kernel, n),
            name="backward",
            out_shape=[shape((dim, ffn), f32), shape((dim, ffn), f32), shape((tokens, dim), bf16)],
            in_specs=[any_space(), full_vmem(), any_space(), any_space(), full_vmem(), full_vmem()],
            out_specs=[full_vmem(), full_vmem(), any_space()],
            scratch_shapes=[big] * 3
            + [pltpu.VMEM((2, size, ffn), bf16), pltpu.VMEM((2, size, ffn), f32)]
            + [dma((count,))] * 2
            + [dma((3, count)), dma((count,)), dma((2,)), dma((2,)), dma((1,))],
            compiler_params=comm_params(3),
        )(gl, xin, hidden, dgelu, w1, w2)

        smem = pl.BlockSpec(memory_space=pltpu.SMEM)
        grad_emb = pl.pallas_call(
            scatter_kernel,
            name="lookup_grad",
            grid=(slice_rows // SCATTER_ROWS,),
            out_shape=shape((slice_rows, dim), f32),
            in_specs=[smem, smem, smem, pl.BlockSpec((dim, SCATTER_ROWS), lambda i: (0, i)), full_vmem()],
            out_specs=pl.BlockSpec((SCATTER_ROWS, dim), lambda i: (i, 0)),
            scratch_shapes=[pltpu.VMEM((tokens, dim), f32)],
            compiler_params=pltpu.CompilerParams(dimension_semantics=("arbitrary",), vmem_limit_bytes=VMEM_BYTES),
        )(starts, sorted_ids, sorted_pos, det, gx)

        mean_loss = (loss[0, :1] / tokens).astype(f32)
        return mean_loss, dw1[None], dw2t.T[None], grad_emb

    return jax.shard_map(
        stage_body,
        mesh=mesh,
        in_specs=(P("dp", None), P("dp", None), P("stage", None), P("stage", None, None), P("stage", None, None)),
        out_specs=(P("dp"), P(("dp", "stage"), None, None), P(("dp", "stage"), None, None), P(("dp", "stage"), None)),
        check_vma=False,
    )
```

time: 4420 us -> 741 us (0.17)
  waiting for transfers between devices: 1690 us -> 0 us
  matrix products: 1030 us -> 0 us
  blocking collectives: 761 us -> 0 us
  Pallas kernels: 0 us -> 668 us
  other arithmetic: 317 us -> 13 us
  local copies, waits for them, and re-layouts: 356 us -> 57.4 us
  starting transfers between devices: 198 us -> 0 us
    psum x35 -> x0, waiting for transfers between devices: 1530 us -> none  [the longest x32 1350 us: head_step(): lax.psum(jnp.einsum('tv,vd->td', grad_logits, emb_rows, preferred_element...]
    dot_general x288 -> x0, matrix products: 1030 us -> none  [the longest x32 309 us: head_step(): jnp.einsum('tv,td->vd', grad_logits, normed_mb, preferred_element_type=jn...]
    pallas_call x0 -> x4, Pallas kernels: none -> 668 us  [the longest x1 304 us: stage_body(): pl.pallas_call(functools.partial(fwd_kernel, n), name='forward', out_shap...]
    psum x32 -> x0, blocking collectives: 400 us -> none  [head_step(): lax.psum(jnp.stack([jnp.sum(exp_logits, axis=1), jnp.sum(jnp.where(is_lab...]
    pmax x32 -> x0, blocking collectives: 361 us -> none  [head_step(): row_max = lax.pmax(jnp.max(logits, axis=1), 'stage')]
    ppermute x78 -> x0, starting transfers between devices: 198 us -> none  [the longest x39 102 us: bwd_tick(): lax.ppermute(grad_in, 'stage', bwd_pairs)]
    ppermute x78 -> x0, waiting for transfers between devices: 159 us -> none  [the longest x39 96.7 us: fwd_tick(): return (lax.ppermute(act_out, 'stage', fwd_pairs), saved_in, last_out)]
    dynamic_update_slice x117 -> x0, other arithmetic: 157 us -> none  [put_slot(): lax.dynamic_update_index_in_dim(store_arr, jnp.where(active, new_value, o...]
  transfers between devices with their start and end apart: 113 -> 0, of which waited for: 109 -> 0; matrix products, arithmetic and copies ran while one was open for 12% -> 0% of each run, Pallas kernels for 0% -> 0%
where the time goes in v1:
time: 741 us
  Pallas kernels  668 us (90%)
  local copies, waits for them, and re-layouts  57.4 us (8%)
  other arithmetic  13 us (2%)
    pallas_call x1, Pallas kernels, stage_body(): pl.pallas_call(functools.partial(fwd_kernel, n), name='forward', out_shap...  304 us
    pallas_call x1, Pallas kernels, stage_body(): pl.pallas_call(functools.partial(head_kernel, n), name='head', out_shape=...  199 us
    pallas_call x1, Pallas kernels, stage_body(): pl.pallas_call(functools.partial(bwd_kernel, n), name='backward', out_sha...  142 us
    unnamed x13, local copies, waits for them, and re-layouts  31.8 us
    gather x1, local copies, waits for them, and re-layouts, stage_body(): jnp.take(emb_rows, jnp.clip(local_tok, 0, slice_rows - 1), axis=0)  22.3 us
    pallas_call x1, Pallas kernels, stage_body(): pl.pallas_call(scatter_kernel, name='lookup_grad', grid=(slice_rows // SC...  21.9 us

profile of v1, /device:TPU:117, one launch (start us, length us, event | category | flops | bytes accessed | tf_op | source)
XLA Modules:
  0.0 740.5 jit_solution(379110264054928067)
XLA Ops:
  0.6 0.7 subtract_clamp_fusion
  1.4 10.5 %copy.18.emb = bf16[6144,576]{1,0:T(8,128)(2,1)} copy(bf16[6144,576]{0,1:T(8,128)(2,1)} %param.7) | data formatting | bytes 14155776 | tf_op args[2]
  11.9 0.0 copy-start.3
  11.9 22.3 %gather_fusion = bf16[4096,576]{1,0:T(8,128)(2,1)} fusion(bf16[6144,576]{1,0:T(8,128)(2,1)} %copy.18.emb, s32[4096]{0:T(1024)S(1)} %broadcast_clamp_fusion), kind=kCustom, calls=%fused_computation | custom fusion | bytes 9453568 | tf_op jit(solution)/shard_map/jit(_take)/gather | solution.py:620
  34.2 0.0 copy-done.3
  34.2 0.0 copy-start.2
  34.2 5.9 select_select_fusion.rows
  40.1 0.0 copy-done.2
  40.1 2.2 copy.19
  42.4 304.1 %forward.1 = (bf16[4096,576]{1,0:T(8,128)(2,1)}, bf16[4096,576]{1,0:T(8,128)(2,1)}, bf16[4096,1536]{1,0:T(8,128)(2,1)}, f32[4096,1536]{1,0:T(8,128)}) custom-call(bf16[4096,576]{1,0:T(8,128)(2,1)} %select_select_fusion.rows, bf16[576,1536]{1,0:T(8,128)(2,1)} %bitcast.27, bf16[1536,576]{1,0:T(8,128)(2,1)} %bitcast.25), custom_call_target="tpu_custom_call" | custom-call | tf_op jit(solution)/shard_map/forward/pallas_call | solution.py:631
  346.5 2.0 copy.21.lab
  348.5 199.3 %head.1 = (f32[576,6144]{1,0:T(8,128)}, bf16[4096,576]{1,0:T(8,128)(2,1)}, f32[8,128]{1,0:T(8,128)}) custom-call(bf16[4096,576]{1,0:T(8,128)(2,1)} %get-tuple-element.16.xl, bf16[6144,576]{1,0:T(8,128)(2,1)} %copy.18.emb, s32[4096,1]{1,0:T(8,128)} %copy.21.lab), custom_call_target="tpu_custom_call" | custom-call | tf_op jit(solution)/shard_map/head/pallas_call | solution.py:647
  547.8 142.3 %backward.1 = (f32[576,1536]{1,0:T(8,128)}, f32[576,1536]{1,0:T(8,128)}, bf16[4096,576]{1,0:T(8,128)(2,1)}) custom-call(bf16[4096,576]{1,0:T(8,128)(2,1)} %get-tuple-element.18.gl, bf16[4096,576]{1,0:T(8,128)(2,1)} %get-tuple-element.19.xin, bf16[4096,1536]{1,0:T(8,128)(2,1)} %get-tuple-element.20.h_in, f32[4096,1536]{1,0:T(8,128)} %get-tuple-element.21.dg_in, ...), custom_call_target="tpu_custom_call" | custom-call | tf_op jit(solution)/shard_map/backward/pallas_call | solution.py:672
  690.1 5.6 sort.15
  695.7 0.7 convert_reduce_fusion.starts
  696.4 21.9 %lookup_grad.1 = f32[6144,576]{1,0:T(8,128)} custom-call(s32[13]{0:T(128)} %convert_reduce_fusion.starts, s32[4096]{0:T(1024)} %get-tuple-element.24.ids, s32[4096]{0:T(1024)} %get-tuple-element.25.pos, f32[576,6144]{1,0:T(8,128)} %get-tuple-element.26.det, bf16[4096,576]{1,0:T(8,128)(2,1)} %get-tuple-element.27.gx), custom_call_target="tpu_custom_call" | custom-call | tf_op jit(solution)/shard_map/lookup_grad/pallas_call | solution.py:686
  718.4 0.0 copy-start.1
  718.4 15.4 %copy.22 = f32[6144,576]{0,1:T(8,128)} copy(f32[6144,576]{1,0:T(8,128)} %lookup_grad.1) | data formatting | bytes 28311552
  733.8 0.0 copy-start
  733.8 1.3 slice.3
  735.8 0.0 copy-done.1
  735.8 1.8 copy.25
  737.6 0.0 copy-done
  737.6 1.8 copy.26
  (6 shorter events, 0.1 us)
Async XLA Ops:
  11.9 22.3 %copy-start.3 = (s32[32,128]{1,0:T(8,128)S(1)}, s32[32,128]{1,0:T(8,128)}, u32[]{:S(2)}) copy-start(s32[32,128]{1,0:T(8,128)} %param.5) | copy-start | bytes 49156
  34.2 5.9 copy-start.2
  718.4 17.4 %copy-start.1 = (f32[576,1536]{1,0:T(8,128)S(1)}, f32[576,1536]{1,0:T(8,128)}, u32[]{:S(2)}) copy-start(f32[576,1536]{1,0:T(8,128)} %get-tuple-element.22) | copy-start | bytes 10616836
  733.8 3.8 copy-start

commit v2 on v1

--- a/solution.py
+++ b/solution.py
@@ -13,7 +13,7 @@
 FWD_ROWS = 128
 BWD_ROWS = 256
 HEAD_ROWS = 512
-HEAD_COLS = 1024
+HEAD_COLS = 2048
 SCATTER_ROWS = 512
 GELU_K = 0.7978845608028654
 GELU_C = 0.044715
@@ -79,7 +79,7 @@
         es[sl(c), :] = total
         even_send(c, dst, recv, dev).start()
 
-    lead = 6
+    lead = 8
 
     @pl.when(odd)
     def _():
@@ -144,7 +144,7 @@
         hidden = (pre * cdf).astype(jnp.bfloat16)
         gb[slot] = cdf + (0.5 * pre) * (1.0 - th * th) * (GELU_K + (3.0 * GELU_K * GELU_C) * sq)
         hb[slot] = hidden
-        out = x.astype(jnp.float32) + jnp.dot(hidden, w2[...], preferred_element_type=jnp.float32)
+        out = x.astype(jnp.float32) + dot_nt(hidden, w2[...])
         y[sl(c), :] = out.astype(jnp.bfloat16)
 
         @pl.when(me < last)
@@ -155,23 +155,15 @@
         def _():
             bcast(y, c, 0, last - 1).start()
 
-            @pl.when(lax.rem(c, 2) == 0)
-            def _():
-                bcast(y, c, 1, 1).start()
-
-            @pl.when(lax.rem(c, 2) == 1)
-            def _():
-                bcast(y, c, 1, last - 2).start()
+            bcast(y, c, 1, 1).start()
+            bcast(y, c, 2, last - 2).start()
 
         h_copy(c, slot).start()
         g_copy(c, slot).start()
 
     def has_next(c):
         up = lax.rem(c, 2) == 0
-        return (up & (me < last - 2)) | (jnp.logical_not(up) & (me > 1))
-
-    def next_relay(c):
-        return me + 2 - 4 * lax.rem(c, 2)
+        return (up & (me == 1)) | (jnp.logical_not(up) & (me == last - 2))
 
     def relay_step(c):
         bcast(xl, c, 0, me).wait_recv()
@@ -179,11 +171,11 @@
 
         @pl.when(has_next(c))
         def _():
-            bcast(xl, c, 1, next_relay(c)).start()
-
-    lag = (last - me) * 2 + 4
-
-    @pl.loop(0, count + 2 * last + 4)
+            bcast(xl, c, 1, 3).start()
+
+    lag = jnp.where(me == 1, 24, jnp.where(me == 3, count, 14))
+
+    @pl.loop(0, 2 * count)
     def _(i):
         @pl.when((me == 2) & (i + lead < count))
         def _():
@@ -233,6 +225,10 @@
         @pl.when((me == last) | (relay & has_next(c)))
         def _():
             bcast(xl, c, 1, me).wait_send()
+
+        @pl.when(me == last)
+        def _():
+            bcast(xl, c, 2, me).wait_send()
 
     for c in (count - 2, count - 1):
         h_copy(c, c % 2).wait()
@@ -249,7 +245,7 @@
     me = lax.axis_index("stage")
     last = n - 1
     tokens, dim = xl.shape
-    slice_rows = emb.shape[0]
+    slice_rows = emb.shape[1]
     size, cols = HEAD_ROWS, HEAD_COLS
     blocks, tiles = tokens // size, slice_rows // cols
     own = size // n
@@ -307,7 +303,7 @@
         labsum[...] = jnp.zeros((size, 128), jnp.float32)
 
     def logits_tile(b, j):
-        logits = dot_nt(nblk[...], emb[tile(j), :])
+        logits = jnp.dot(nblk[...], emb[:, tile(j)], preferred_element_type=jnp.float32)
         row_max = jnp.max(logits, axis=1, keepdims=True)
         exps = jnp.exp((logits - row_max) * scale)
         probs[lax.rem(b, 2), :, tile(j)] = exps.astype(jnp.bfloat16)
@@ -344,7 +340,7 @@
         factor = jnp.sum(jnp.where(lane == j, cmat[...], 0.0), axis=1, keepdims=True)
         exps = probs[lax.rem(b, 2), :, tile(j)].astype(jnp.float32)
         dlog = (exps * factor - jnp.where(label_mask(b, j), scale, 0.0)).astype(jnp.bfloat16)
-        gn[...] += jnp.dot(dlog, emb[tile(j), :], preferred_element_type=jnp.float32)
+        gn[...] += dot_nt(dlog, emb[:, tile(j)])
         det[:, tile(j)] += jnp.dot(ntr[lax.rem(b, 3)], dlog, preferred_element_type=jnp.float32)
 
     def wait_grad_sends(b):
@@ -503,7 +499,7 @@
             grad_send(c, me).wait_recv()
 
         grad = gin[sl(c), :]
-        grad_hidden = dot_nt(grad, w2[...])
+        grad_hidden = jnp.dot(grad, w2[...], preferred_element_type=jnp.float32)
         grad_pre = (grad_hidden * gb[slot]).astype(jnp.bfloat16)
         grad_in = grad.astype(jnp.float32) + dot_nt(grad_pre, w1[...])
         gout[sl(c), :] = grad_in.astype(jnp.bfloat16)
@@ -529,9 +525,9 @@
         def _():
             bcast(gall, c, 1, 4).start()
 
-    lag = me + 2
-
-    @pl.loop(0, count + n)
+    lag = jnp.where(me == 2, 6, jnp.where(me == 4, 11, 12))
+
+    @pl.loop(0, count + 12)
     def _(i):
         @pl.when(i < count)
         def _():
@@ -578,22 +574,23 @@
             bcast(gall, c, 2, me).wait_send()
 
 
-def scatter_kernel(starts, ids, pos, det, gx, out, grads):
+def scatter_kernel(starts, ids, pos, det, gx, out, grads, acc):
     blk = pl.program_id(0)
 
     @pl.when(blk == 0)
     def _():
         grads[...] = gx[...].astype(jnp.float32)
 
-    out[...] = det[...].T
+    acc[...] = jnp.zeros_like(acc)
     base = blk * SCATTER_ROWS
 
     def add_row(k, carry):
         row = pl.ds(ids[k] - base, 1)
-        out[row, :] = out[row, :] + grads[pl.ds(pos[k], 1), :]
+        acc[row, :] = acc[row, :] + grads[pl.ds(pos[k], 1), :]
         return carry
 
     lax.fori_loop(starts[blk], starts[blk + 1], add_row, 0)
+    out[...] = det[...] + acc[...].T
 
 
 def comm_params(collective_id):
@@ -611,7 +608,7 @@
         micro_count, micro_tokens = token_ids.shape
         tokens = micro_count * micro_tokens
         slice_rows, dim = emb_rows.shape
-        w1, w2 = w_in[0], w_out[0]
+        w1, w2 = w_in[0], w_out[0].T
         ffn = w1.shape[1]
         row_start = stage_idx * slice_rows
 
@@ -637,7 +634,7 @@
             scratch_shapes=[big] * 7
             + [pltpu.VMEM((2, size, ffn), bf16), pltpu.VMEM((2, size, ffn), f32)]
             + [dma((count,))] * 6
-            + [dma((2, count)), dma((count,)), dma((2,)), dma((2,)), dma((2,))],
+            + [dma((3, count)), dma((count,)), dma((2,)), dma((2,)), dma((2,))],
             compiler_params=comm_params(1),
         )(rows, w1, w2)
 
@@ -666,7 +663,7 @@
             + [dma((blocks, n))] * 4
             + [dma((blocks,)), dma((blocks, n))],
             compiler_params=comm_params(2),
-        )(xl, emb_rows, local_lab)
+        )(xl, emb_rows.T, local_lab)
 
         size, count = BWD_ROWS, tokens // BWD_ROWS
         dw1, dw2t, gx = pl.pallas_call(
@@ -687,15 +684,15 @@
             scatter_kernel,
             name="lookup_grad",
             grid=(slice_rows // SCATTER_ROWS,),
-            out_shape=shape((slice_rows, dim), f32),
+            out_shape=shape((dim, slice_rows), f32),
             in_specs=[smem, smem, smem, pl.BlockSpec((dim, SCATTER_ROWS), lambda i: (0, i)), full_vmem()],
-            out_specs=pl.BlockSpec((SCATTER_ROWS, dim), lambda i: (i, 0)),
-            scratch_shapes=[pltpu.VMEM((tokens, dim), f32)],
+            out_specs=pl.BlockSpec((dim, SCATTER_ROWS), lambda i: (0, i)),
+            scratch_shapes=[pltpu.VMEM((tokens, dim), f32), pltpu.VMEM((SCATTER_ROWS, dim), f32)],
             compiler_params=pltpu.CompilerParams(dimension_semantics=("arbitrary",), vmem_limit_bytes=VMEM_BYTES),
         )(starts, sorted_ids, sorted_pos, det, gx)
 
         mean_loss = (loss[0, :1] / tokens).astype(f32)
-        return mean_loss, dw1[None], dw2t.T[None], grad_emb
+        return mean_loss, dw1[None], dw2t.T[None], grad_emb.T
 
     return jax.shard_map(
         stage_body,

time: 741 us -> 521 us (0.70)
  Pallas kernels: 668 us -> 463 us
  local copies, waits for them, and re-layouts: 57.4 us -> 41.8 us
    pallas_call x1, Pallas kernels: 304 us -> 122 us  [stage_body(): pl.pallas_call(functools.partial(fwd_kernel, n), name='forward', out_shap...]
    pallas_call x1, Pallas kernels: 142 us -> 124 us  [stage_body(): pl.pallas_call(functools.partial(bwd_kernel, n), name='backward', out_sha...]
    unnamed x13 -> x9, local copies, waits for them, and re-layouts: 31.8 us -> 16.5 us
where the time goes in v2:
time: 521 us; the launch traced here: 520 us
  Pallas kernels  463 us (89%)
  local copies, waits for them, and re-layouts  41.8 us (8%)
  other arithmetic  12.3 us (2%)
    pallas_call x1, Pallas kernels, stage_body(): pl.pallas_call(functools.partial(head_kernel, n), name='head', out_shape=...  196 us
    pallas_call x1, Pallas kernels, stage_body(): pl.pallas_call(functools.partial(bwd_kernel, n), name='backward', out_sha...  124 us
    pallas_call x1, Pallas kernels, stage_body(): pl.pallas_call(functools.partial(fwd_kernel, n), name='forward', out_shap...  122 us
    gather x1, local copies, waits for them, and re-layouts, stage_body(): jnp.take(emb_rows, jnp.clip(local_tok, 0, slice_rows - 1), axis=0)  22.2 us
    pallas_call x1, Pallas kernels, stage_body(): pl.pallas_call(scatter_kernel, name='lookup_grad', grid=(slice_rows // SC...  21.4 us
    unnamed x9, local copies, waits for them, and re-layouts  16.5 us

profile of v2, /device:TPU:117, one launch (start us, length us, event | category | flops | bytes accessed | tf_op | source)
XLA Modules:
  0.0 519.7 jit_solution(1415035990849278840)
XLA Ops:
  0.6 0.0 copy-start.1
  0.6 0.0 copy-start.2
  0.7 10.5 %copy.12 = bf16[6144,576]{1,0:T(8,128)(2,1)} copy(bf16[6144,576]{0,1:T(8,128)(2,1)} %param.7) | data formatting | bytes 14155776 | tf_op args[2]
  11.1 0.0 copy-done.1
  11.1 0.0 copy-done.2
  11.2 22.2 %gather_fusion = bf16[4096,576]{1,0:T(8,128)(2,1)} fusion(bf16[6144,576]{1,0:T(8,128)(2,1)} %copy.12, s32[4096]{0:T(1024)S(1)} %broadcast_clamp_fusion), kind=kCustom, calls=%fused_computation | custom fusion | bytes 9453568 | tf_op jit(solution)/shard_map/jit(_take)/gather | solution.py:617
  33.4 5.8 %select_select_fusion.rows = bf16[4096,576]{1,0:T(8,128)(2,1)} fusion(bf16[4096,576]{1,0:T(8,128)(2,1)} %gather_fusion, pred[4096]{0:T(1024)(128)(4,1)S(1)} %get-tuple-element.29, pred[4096]{0:T(1024)(128)(4,1)S(1)} %get-tuple-element.28), kind=kLoop, calls=%fused_computation.1 | loop fusion | flops 4718592 | bytes 9445376 | tf_op jit(solution)/shard_map/jit(_where)/select_n | solution.py:618
  39.2 121.7 %forward.1 = (bf16[4096,576]{1,0:T(8,128)(2,1)}, bf16[4096,576]{1,0:T(8,128)(2,1)}, bf16[4096,1536]{1,0:T(8,128)(2,1)}, f32[4096,1536]{1,0:T(8,128)}) custom-call(bf16[4096,576]{1,0:T(8,128)(2,1)} %select_select_fusion.rows, bf16[576,1536]{1,0:T(8,128)(2,1)} %bitcast.31, bf16[576,1536]{1,0:T(8,128)(2,1)} %bitcast.33), custom_call_target="tpu_custom_call" | custom-call | tf_op jit(solution)/shard_map/forward/pallas_call | solution.py:628
  160.9 2.0 copy.13.lab
  162.9 196.3 %head.1 = (f32[576,6144]{1,0:T(8,128)}, bf16[4096,576]{1,0:T(8,128)(2,1)}, f32[8,128]{1,0:T(8,128)}) custom-call(bf16[4096,576]{1,0:T(8,128)(2,1)} %get-tuple-element.16.xl, bf16[576,6144]{1,0:T(8,128)(2,1)} %bitcast.29, s32[4096,1]{1,0:T(8,128)} %copy.13.lab), custom_call_target="tpu_custom_call" | custom-call | tf_op jit(solution)/shard_map/head/pallas_call | solution.py:644
  359.3 1.2 slice.3
  361.1 123.7 %backward.1 = (f32[576,1536]{1,0:T(8,128)}, f32[576,1536]{1,0:T(8,128)}, bf16[4096,576]{1,0:T(8,128)(2,1)}) custom-call(bf16[4096,576]{1,0:T(8,128)(2,1)} %get-tuple-element.18.gl, bf16[4096,576]{1,0:T(8,128)(2,1)} %get-tuple-element.19.xin, bf16[4096,1536]{1,0:T(8,128)(2,1)} %get-tuple-element.20.h_in, f32[4096,1536]{1,0:T(8,128)} %get-tuple-element.21.dg_in, ...), custom_call_target="tpu_custom_call" | custom-call | tf_op jit(solution)/shard_map/backward/pallas_call | solution.py:669
  484.8 0.8 convert_reduce_fusion.starts
  485.7 5.6 %sort.15 = (s32[4096]{0:T(1024)}, s32[4096]{0:T(1024)}) sort(s32[4096]{0:T(1024)S(1)} %bitcast_select_fusion, s32[4096]{0:T(1024)S(1)} %iota.9), dimensions={0}, to_apply=%region_1.2 | sort | flops 49152 | bytes 65536 | tf_op jit(solution)/shard_map/sort | solution.py:622
  491.2 21.4 %lookup_grad.1 = f32[576,6144]{1,0:T(8,128)} custom-call(s32[13]{0:T(128)} %convert_reduce_fusion.starts, s32[4096]{0:T(1024)} %get-tuple-element.24.ids, s32[4096]{0:T(1024)} %get-tuple-element.25.pos, f32[576,6144]{1,0:T(8,128)} %get-tuple-element.26.det, bf16[4096,576]{1,0:T(8,128)(2,1)} %get-tuple-element.27.gx), custom_call_target="tpu_custom_call" | custom-call | tf_op jit(solution)/shard_map/lookup_grad/pallas_call | solution.py:683
  512.6 0.0 copy-start
  512.6 4.2 copy.16
  516.8 0.0 copy-done
  516.8 1.8 copy.17
  (7 shorter events, 0.1 us)
Async XLA Ops:
  0.6 10.5 %copy-start.1 = (s32[32,128]{1,0:T(8,128)S(1)}, s32[32,128]{1,0:T(8,128)}, u32[]{:S(2)}) copy-start(s32[32,128]{1,0:T(8,128)} %param.5) | copy-start | bytes 49156
  0.6 10.5 %copy-start.2 = (s32[32,128]{1,0:T(8,128)S(1)}, s32[32,128]{1,0:T(8,128)}, u32[]{:S(2)}) copy-start(s32[32,128]{1,0:T(8,128)} %param.6) | copy-start | bytes 49156
  512.6 4.2 copy-start

commit v3 on v2

--- a/solution.py
+++ b/solution.py
@@ -70,16 +70,36 @@
     def even_send(c, dst, recv, dev):
         return remote(es.at[sl(c)], dst.at[sl(c)], e_send.at[c], recv.at[c], dev)
 
-    def combine_and_send(c, has_eb, dst, recv, dev):
+    def combine_two(c):
         even_send(c, ea, ea_recv, me).wait_recv()
-        total = rows[sl(c), :] + ea[sl(c), :]
-        if has_eb:
+        even_send(c, eb, eb_recv, me).wait_recv()
+        es[sl(c), :] = rows[sl(c), :] + ea[sl(c), :] + eb[sl(c), :]
+        even_send(c, eb, eb_recv, 0).start()
+
+    def combine_four(c):
+        even_send(c, ea, ea_recv, me).wait_recv()
+        es[sl(c), :] = rows[sl(c), :] + ea[sl(c), :]
+
+        @pl.when(lax.rem(c, 2) == 1)
+        def _():
             even_send(c, eb, eb_recv, me).wait_recv()
-            total = total + eb[sl(c), :]
-        es[sl(c), :] = total
-        even_send(c, dst, recv, dev).start()
-
-    lead = 8
+            es[sl(c), :] = es[sl(c), :] + eb[sl(c), :]
+
+        even_send(c, eb, eb_recv, 2).start()
+
+    def combine_six(c):
+        even_send(c, ea, ea_recv, me).wait_recv()
+        es[sl(c), :] = rows[sl(c), :] + ea[sl(c), :]
+
+        @pl.when(lax.rem(c, 2) == 0)
+        def _():
+            even_send(c, ec, ec_recv, 0).start()
+
+        @pl.when(lax.rem(c, 2) == 1)
+        def _():
+            even_send(c, eb, eb_recv, 4).start()
+
+    lead, lead_four = 8, 16
 
     @pl.when(odd)
     def _():
@@ -89,21 +109,21 @@
 
     @pl.when(me == 4)
     def _():
+        @pl.loop(0, lead_four)
+        def _(c):
+            combine_four(c)
+
+    @pl.when(me == 6)
+    def _():
         @pl.loop(0, count)
         def _(c):
-            combine_and_send(c, False, eb, eb_recv, 2)
-
-    @pl.when(me == 6)
-    def _():
-        @pl.loop(0, count)
-        def _(c):
-            combine_and_send(c, False, ec, ec_recv, 0)
+            combine_six(c)
 
     @pl.when(me == 2)
     def _():
         @pl.loop(0, lead)
         def _(c):
-            combine_and_send(c, True, eb, eb_recv, 0)
+            combine_two(c)
 
     def fwd_send(c):
         return remote(y.at[sl(c)], xin.at[sl(c)], f_send.at[c], x_recv.at[c], me + 1)
@@ -124,8 +144,12 @@
         def _():
             even_send(c, ea, ea_recv, me).wait_recv()
             even_send(c, eb, eb_recv, me).wait_recv()
-            even_send(c, ec, ec_recv, me).wait_recv()
-            xin[sl(c), :] = (rows[sl(c), :] + ea[sl(c), :]) + (eb[sl(c), :] + ec[sl(c), :])
+            xin[sl(c), :] = (rows[sl(c), :] + ea[sl(c), :]) + eb[sl(c), :]
+
+            @pl.when(lax.rem(c, 2) == 0)
+            def _():
+                even_send(c, ec, ec_recv, me).wait_recv()
+                xin[sl(c), :] = xin[sl(c), :] + ec[sl(c), :]
 
         @pl.when(me > 0)
         def _():
@@ -179,7 +203,11 @@
     def _(i):
         @pl.when((me == 2) & (i + lead < count))
         def _():
-            combine_and_send(i + lead, True, eb, eb_recv, 0)
+            combine_two(i + lead)
+
+        @pl.when((me == 4) & (i + lead_four < count))
+        def _():
+            combine_four(i + lead_four)
 
         @pl.when(i < count)
         def _():
@@ -574,8 +602,31 @@
             bcast(gall, c, 2, me).wait_send()
 
 
-def scatter_kernel(starts, ids, pos, det, gx, out, grads, acc):
+def lookup_kernel(starts, ids, pos, emb, out, table, acc):
     blk = pl.program_id(0)
+
+    @pl.when(blk == 0)
+    def _():
+        acc[...] = jnp.zeros_like(acc)
+
+    table[...] = emb[...].astype(jnp.float32).T
+    base = blk * SCATTER_ROWS
+
+    def take_row(k, carry):
+        acc[pl.ds(pos[k], 1), :] = table[pl.ds(ids[k] - base, 1), :]
+        return carry
+
+    lax.fori_loop(starts[blk], starts[blk + 1], take_row, 0)
+
+    @pl.when(blk == pl.num_programs(0) - 1)
+    def _():
+        out[...] = acc[...].astype(jnp.bfloat16)
+
+
+def scatter_kernel(starts, ids, pos, det, gx, dw1, dw2, out, dw1_out, dw2_out, grads, acc):
+    blk = pl.program_id(0)
+    dw1_out[...] = dw1[...]
+    dw2_out[...] = dw2[...]
 
     @pl.when(blk == 0)
     def _():
@@ -614,14 +665,27 @@
 
         local_tok = token_ids.reshape(tokens) - row_start
         tok_here = (local_tok >= 0) & (local_tok < slice_rows)
-        looked_up = jnp.take(emb_rows, jnp.clip(local_tok, 0, slice_rows - 1), axis=0)
-        rows = jnp.where(tok_here[:, None], looked_up, 0)
         local_lab = label_ids.reshape(tokens, 1) - row_start
 
         keys = jnp.where(tok_here, local_tok, slice_rows)
         sorted_ids, sorted_pos = lax.sort((keys, lax.iota(jnp.int32, tokens)), num_keys=1, is_stable=False)
         edges = lax.iota(jnp.int32, slice_rows // SCATTER_ROWS + 1) * SCATTER_ROWS
         starts = jnp.sum((keys[None, :] < edges[:, None]).astype(jnp.int32), axis=1)
+
+        smem = pl.BlockSpec(memory_space=pltpu.SMEM)
+        grid = slice_rows // SCATTER_ROWS
+        emb_block = pl.BlockSpec((dim, SCATTER_ROWS), lambda i: (0, i))
+        grid_params = pltpu.CompilerParams(dimension_semantics=("arbitrary",), vmem_limit_bytes=VMEM_BYTES)
+        rows = pl.pallas_call(
+            lookup_kernel,
+            name="lookup",
+            grid=(grid,),
+            out_shape=shape((tokens, dim), bf16),
+            in_specs=[smem, smem, smem, emb_block],
+            out_specs=full_vmem(),
+            scratch_shapes=[pltpu.VMEM((SCATTER_ROWS, dim), f32), pltpu.VMEM((tokens, dim), f32)],
+            compiler_params=grid_params,
+        )(starts, sorted_ids, sorted_pos, emb_rows.T)
 
         size, count = FWD_ROWS, tokens // FWD_ROWS
         big = pltpu.VMEM((tokens, dim), bf16)
@@ -679,17 +743,17 @@
             compiler_params=comm_params(3),
         )(gl, xin, hidden, dgelu, w1, w2)
 
-        smem = pl.BlockSpec(memory_space=pltpu.SMEM)
-        grad_emb = pl.pallas_call(
+        dw_block = pl.BlockSpec((dim // grid, ffn), lambda i: (i, 0))
+        grad_emb, dw1, dw2t = pl.pallas_call(
             scatter_kernel,
             name="lookup_grad",
-            grid=(slice_rows // SCATTER_ROWS,),
-            out_shape=shape((dim, slice_rows), f32),
-            in_specs=[smem, smem, smem, pl.BlockSpec((dim, SCATTER_ROWS), lambda i: (0, i)), full_vmem()],
-            out_specs=pl.BlockSpec((dim, SCATTER_ROWS), lambda i: (0, i)),
+            grid=(grid,),
+            out_shape=[shape((dim, slice_rows), f32), shape((dim, ffn), f32), shape((dim, ffn), f32)],
+            in_specs=[smem, smem, smem, emb_block, full_vmem(), dw_block, dw_block],
+            out_specs=[emb_block, dw_block, dw_block],
             scratch_shapes=[pltpu.VMEM((tokens, dim), f32), pltpu.VMEM((SCATTER_ROWS, dim), f32)],
-            compiler_params=pltpu.CompilerParams(dimension_semantics=("arbitrary",), vmem_limit_bytes=VMEM_BYTES),
-        )(starts, sorted_ids, sorted_pos, det, gx)
+            compiler_params=grid_params,
+        )(starts, sorted_ids, sorted_pos, det, gx, dw1, dw2t)
 
         mean_loss = (loss[0, :1] / tokens).astype(f32)
         return mean_loss, dw1[None], dw2t.T[None], grad_emb.T

time: 521 us -> 485 us (0.931)
  local copies, waits for them, and re-layouts: 41.8 us -> 3.16 us
  Pallas kernels: 463 us -> 472 us
  other arithmetic: 12.3 us -> 7.05 us
    gather x1 -> x0, local copies, waits for them, and re-layouts: 22.2 us -> none  [stage_body(): jnp.take(emb_rows, jnp.clip(local_tok, 0, slice_rows - 1), axis=0)]
    pallas_call x1 -> x2, Pallas kernels: 21.4 us -> 41.4 us  [the longest x1 24.7 us: stage_body(): pl.pallas_call(scatter_kernel, name='lookup_grad', grid=(grid,), out_shap...]
    unnamed x9 -> x2, local copies, waits for them, and re-layouts: 16.5 us -> 0.01 us
    pallas_call x1, Pallas kernels: 122 us -> 114 us  [stage_body(): pl.pallas_call(functools.partial(fwd_kernel, n), name='forward', out_shap...]
    select_n x2 -> x0, other arithmetic: 5.85 us -> none  [the longest x1 5.83 us: stage_body(): rows = jnp.where(tok_here[:, None], looked_up, 0)]
where the time goes in v3:
time: 485 us
  Pallas kernels  472 us (97%)
  other arithmetic  7.05 us (1%)
    pallas_call x1, Pallas kernels, stage_body(): pl.pallas_call(functools.partial(head_kernel, n), name='head', out_shape=...  193 us
    pallas_call x1, Pallas kernels, stage_body(): pl.pallas_call(functools.partial(bwd_kernel, n), name='backward', out_sha...  124 us
    pallas_call x1, Pallas kernels, stage_body(): pl.pallas_call(functools.partial(fwd_kernel, n), name='forward', out_shap...  114 us
    pallas_call x1, Pallas kernels, stage_body(): pl.pallas_call(scatter_kernel, name='lookup_grad', grid=(grid,), out_shap...  24.7 us
    pallas_call x1, Pallas kernels, stage_body(): pl.pallas_call(lookup_kernel, name='lookup', grid=(grid,), out_shape=shap...  16.7 us

profile of v3, /device:TPU:117, one launch (start us, length us, event | category | flops | bytes accessed | tf_op | source)
XLA Modules:
  0.0 484.8 jit_solution(9255464714567317984)
XLA Ops:
  0.6 0.7 bitcast_select_fusion
  1.4 0.7 convert_reduce_fusion.starts
  2.1 5.6 %sort.15 = (s32[4096]{0:T(1024)}, s32[4096]{0:T(1024)}) sort(s32[4096]{0:T(1024)S(1)} %bitcast_select_fusion, s32[4096]{0:T(1024)S(1)} %iota.9), dimensions={0}, to_apply=%region_1.2 | sort | flops 49152 | bytes 65536 | tf_op jit(solution)/shard_map/sort | solution.py:671
  7.7 16.7 %lookup.1.rows = bf16[4096,576]{1,0:T(8,128)(2,1)} custom-call(s32[13]{0:T(128)} %convert_reduce_fusion.starts, s32[4096]{0:T(1024)} %get-tuple-element.19.ids, s32[4096]{0:T(1024)} %get-tuple-element.20.pos, bf16[576,6144]{1,0:T(8,128)(2,1)} %bitcast.22), custom_call_target="tpu_custom_call" | custom-call | tf_op jit(solution)/shard_map/lookup/pallas_call | solution.py:679
  24.3 0.0 copy-start
  24.3 114.3 %forward.1 = (bf16[4096,576]{1,0:T(8,128)(2,1)}, bf16[4096,576]{1,0:T(8,128)(2,1)}, bf16[4096,1536]{1,0:T(8,128)(2,1)}, f32[4096,1536]{1,0:T(8,128)}) custom-call(bf16[4096,576]{1,0:T(8,128)(2,1)} %lookup.1.rows, bf16[576,1536]{1,0:T(8,128)(2,1)} %bitcast.24, bf16[576,1536]{1,0:T(8,128)(2,1)} %bitcast.26), custom_call_target="tpu_custom_call" | custom-call | tf_op jit(solution)/shard_map/forward/pallas_call | solution.py:692
  138.7 0.0 copy-done
  138.7 2.0 copy.10.lab
  140.7 192.7 %head.1 = (f32[576,6144]{1,0:T(8,128)}, bf16[4096,576]{1,0:T(8,128)(2,1)}, f32[8,128]{1,0:T(8,128)}) custom-call(bf16[4096,576]{1,0:T(8,128)(2,1)} %get-tuple-element.21.xl, bf16[576,6144]{1,0:T(8,128)(2,1)} %bitcast.23, s32[4096,1]{1,0:T(8,128)} %copy.10.lab), custom_call_target="tpu_custom_call" | custom-call | tf_op jit(solution)/shard_map/head/pallas_call | solution.py:708
  333.4 1.2 slice.3
  335.2 123.7 %backward.1 = (f32[576,1536]{1,0:T(8,128)}, f32[576,1536]{1,0:T(8,128)}, bf16[4096,576]{1,0:T(8,128)(2,1)}) custom-call(bf16[4096,576]{1,0:T(8,128)(2,1)} %get-tuple-element.24.gl, bf16[4096,576]{1,0:T(8,128)(2,1)} %get-tuple-element.25.xin, bf16[4096,1536]{1,0:T(8,128)(2,1)} %get-tuple-element.26.h_in, f32[4096,1536]{1,0:T(8,128)} %get-tuple-element.27.dg_in, ...), custom_call_target="tpu_custom_call" | custom-call | tf_op jit(solution)/shard_map/backward/pallas_call | solution.py:733
  458.9 24.7 %lookup_grad.1 = (f32[576,6144]{1,0:T(8,128)}, f32[576,1536]{1,0:T(8,128)}, f32[576,1536]{1,0:T(8,128)}) custom-call(s32[13]{0:T(128)} %convert_reduce_fusion.starts, s32[4096]{0:T(1024)} %get-tuple-element.19.ids, s32[4096]{0:T(1024)} %get-tuple-element.20.pos, f32[576,6144]{1,0:T(8,128)} %get-tuple-element.23.det, bf16[4096,576]{1,0:T(8,128)(2,1)} %get-tuple-element.28.gx, ...), custom_call_target="tpu_custom_call" | custom-call | tf_op jit(solution)/shard_map/lookup_grad/pallas_call | solution.py:747
  (3 shorter events, 0.0 us)
Async XLA Ops:
  24.3 114.3 %copy-start = (s32[32,128]{1,0:T(8,128)S(1)}, s32[32,128]{1,0:T(8,128)}, u32[]{:S(2)}) copy-start(s32[32,128]{1,0:T(8,128)} %param.6) | copy-start | bytes 49156
